TPU v7x, 64 devices: a 2x2x8 block of a 4x4x8 slice. The times are simulated.
64 devices in a mesh: dp: 4 (over x, y), tp: 16 (over z, core).
Axes of the slice: x: 2, y: 2, z: 8, core: 2. Of those that a mesh axis runs over, the one named last changes fastest.
The devices are a block of a 4x4x8 slice.
Arguments:
- x_in: bfloat16 [8192, 2048], P(('dp', 'tp')), parts along dimension 0
- grad_y: bfloat16 [8192, 2048], P(('dp', 'tp')), parts along dimension 0
- norm_gain: float32 [2, 2048], replicated
- w_qkv: bfloat16 [2, 2048, 6144], P(None, None, 'tp')
- w_out: bfloat16 [2, 2048, 2048], P(None, 'tp')
- w_gate: bfloat16 [2, 2048, 8192], P(None, None, 'tp')
- w_up: bfloat16 [2, 2048, 8192], P(None, None, 'tp')
- w_down: bfloat16 [2, 8192, 2048], P(None, 'tp')
Outputs:
- output 1: bfloat16 [8192, 2048], P(('dp', 'tp')), parts along dimension 0
- output 2: float32 [8, 2048], P('dp'), parts along dimension 0
- output 3: bfloat16 [8, 2048, 6144], P('dp', None, 'tp'), parts along dimension 0
- output 4: bfloat16 [8, 2048, 2048], P('dp', 'tp'), parts along dimension 0
- output 5: bfloat16 [8, 2048, 8192], P('dp', None, 'tp'), parts along dimension 0
- output 6: bfloat16 [8, 2048, 8192], P('dp', None, 'tp'), parts along dimension 0
- output 7: bfloat16 [8, 8192, 2048], P('dp', 'tp'), parts along dimension 0
There are 4 independent parts. A program takes and returns all parts, laid end to end along the dimension named above; an argument that names none is the same for every part.
All inputs are finite; a program needn't handle non-finite values.
Results may differ from a plain program's by a relative error of at most 0.0158805.
Values are sent between devices in bfloat16 or wider.
A program may use at most 768 MiB of HBM per device.

v0:
```python
import functools

import jax
import jax.numpy as jnp
import numpy as np
from jax import lax
from jax.experimental import pallas as pl
from jax.experimental.pallas import tpu as pltpu
from jax.sharding import PartitionSpec as P

HEAD_DIM = 128
NORM_EPS = 1e-5
ROPE_BASE = 10000.0
MESH = pl.DeviceIdType.MESH
NP = 4
F32 = jnp.float32
BF16 = jnp.bfloat16


def dot_nn(a, b):
    return lax.dot_general(a, b, (((1,), (0,)), ((), ())), preferred_element_type=F32)


def dot_nt(a, b):
    return lax.dot_general(a, b, (((1,), (1,)), ((), ())), preferred_element_type=F32)


def dot_tn(a, b):
    return lax.dot_general(a, b, (((0,), (0,)), ((), ())), preferred_element_type=F32)


def not_below_zero(index):
    return jnp.maximum(index, 0)


def row_mean(values):
    return jnp.mean(values, axis=-1, keepdims=True)


def row_sum(values):
    return jnp.sum(values, axis=-1, keepdims=True)


def loop_from(first, last, body):
    def step(index, carry):
        body(index)
        return carry
    lax.fori_loop(first, last, step, 0)


def loop(count, body):
    loop_from(0, count, body)


def aligned(index, size):
    return pl.multiple_of(index, size)


class Place:
    def __init__(self, tp_size):
        index = lax.axis_index('tp')
        self.ring = tp_size // 2
        self.half = self.ring // 2
        self.core = lax.rem(index, 2)
        self.chip = lax.div(index, 2)
        self.right = self.peer(1)
        self.left = self.peer(-1)
        self.mate = {'tp': self.chip * 2 + 1 - self.core}

    def peer(self, step):
        return {'tp': self.near(step) * 2 + self.core}

    def near(self, step):
        return lax.rem(self.chip + step + self.ring, self.ring)

    def arrive(self):
        peers = [self.right, self.left, self.mate]
        for peer in peers:
            pl.semaphore_signal(pltpu.get_barrier_semaphore(), inc=1, device_id=peer, device_id_type=MESH)
        return len(peers)


class Gather:
    def __init__(self, place, buf, shard_rows, sems):
        self.place, self.buf, self.shard = place, buf, shard_rows
        self.rows = shard_rows // NP
        self.events = (place.half - 1) * NP + NP // 2
        self.send, self.recv_r, self.recv_l, self.recv_m = sems

    @staticmethod
    def scratch(half):
        events = (half - 1) * NP + NP // 2
        return [pltpu.SemaphoreType.DMA(())] + [pltpu.SemaphoreType.DMA((n,)) for n in (events, events, 2 * half)]

    def view(self, chip, core, piece):
        start = (chip * 2 + core) * self.shard + piece * self.rows
        return self.buf.at[pl.ds(aligned(start, self.rows), self.rows)]

    def own_rows(self):
        start = (self.place.chip * 2 + self.place.core) * self.shard
        return pl.ds(aligned(start, self.shard), self.shard)

    def copy(self, source, view, recv, to):
        return pltpu.make_async_remote_copy(source, view, self.send, recv, to, MESH)

    def to_right(self, event, view):
        return self.copy(view, view, self.recv_r.at[event], self.place.right)

    def to_left(self, event, view):
        return self.copy(view, view, self.recv_l.at[event], self.place.left)

    def group(self, event, rightward):
        half = self.place.half
        return lax.select(event >= (half - 1) * NP, 2 * half - 1, lax.div(event, NP) + (half if rightward else 1))

    def to_mate(self, group, view):
        return self.copy(view, view, self.recv_m.at[group], self.place.mate)

    def start(self):
        place = self.place
        for piece in range(NP):
            self.to_right(piece, self.view(place.chip, place.core, piece)).start()
            self.to_left(piece, self.view(place.chip, place.core, NP - 1 - piece)).start()
        for piece in range(NP):
            self.to_mate(0, self.view(place.chip, place.core, piece)).start()

    def views(self, event):
        step = lax.div(event, NP) + 1
        piece = lax.rem(event, NP)
        from_left = self.view(self.place.near(-step), self.place.core, piece)
        from_right = self.view(self.place.near(step), self.place.core, NP - 1 - piece)
        return from_left, from_right

    def event(self, event, forward=None):
        from_left, from_right = self.views(event)
        self.to_right(event, from_left).wait_recv()
        self.pass_on(event, forward, lambda: self.to_right(event + NP, from_left).start())
        self.to_mate(self.group(event, False), from_left).start()
        self.to_left(event, from_right).wait_recv()
        self.pass_on(event, forward, lambda: self.to_left(event + NP, from_right).start())
        self.to_mate(self.group(event, True), from_right).start()

    def forward(self, event):
        from_left, from_right = self.views(event)
        self.to_right(event + NP, from_left).start()
        self.to_left(event + NP, from_right).start()

    def side_view(self, side, which, piece):
        return side.at[which, pl.ds(aligned(piece * self.rows, self.rows), self.rows)]

    def start_side(self, side):
        for piece in range(NP):
            last = NP - 1 - piece
            self.copy(self.side_view(side, 0, piece), self.side_view(side, 1, piece), self.recv_r.at[piece], self.place.right).start()
            self.copy(self.side_view(side, 0, last), self.side_view(side, 2, last), self.recv_l.at[piece], self.place.left).start()

    def adopt_side(self, side):
        place = self.place

        def body(piece):
            last = NP - 1 - piece
            from_left, from_right = self.side_view(side, 1, piece), self.side_view(side, 2, last)
            self.to_right(piece, from_left).wait_recv()
            self.to_left(piece, from_right).wait_recv()
            to_left, to_right = self.views(piece)
            for source, view, group in ((self.side_view(side, 0, piece), self.view(place.chip, place.core, piece), 0),
                                        (from_left, to_left, 1), (from_right, to_right, place.half)):
                self.copy(source, view, self.recv_m.at[group], place.mate).start()
        loop(NP, body)
        for which, step in ((0, 0), (1, -1), (2, 1)):
            start = (place.near(step) * 2 + place.core) * self.shard
            self.buf[pl.ds(aligned(start, self.shard), self.shard)] = side[which]

    def forward_side(self, side, event):
        from_left, from_right = self.views(event)
        later = event + NP
        self.copy(self.side_view(side, 1, event), from_left, self.recv_r.at[later], self.place.right).start()
        self.copy(self.side_view(side, 2, NP - 1 - event), from_right, self.recv_l.at[later], self.place.left).start()

    def pass_on(self, event, forward, send):
        if forward is None:
            pl.when(event + NP < self.events)(send)
        elif forward:
            send()

    def mate_wait(self, group, step):
        start = (self.place.near(step) * 2 + 1 - self.place.core) * self.shard
        self.to_mate(group, self.buf.at[pl.ds(aligned(start, self.shard), self.shard)]).wait_recv()

    def mate_wait_last(self):
        self.mate_wait(2 * self.place.half - 1, self.place.half)

    def mate_wait_chip(self, distance, rightward):
        far = lax.select(rightward, distance + self.place.half - 1, distance)
        self.mate_wait(lax.select(distance == 0, 0, far), lax.select(rightward, distance, -distance))

    def mate_wait_all(self):
        self.mate_wait(0, 0)

        def body(turn):
            self.mate_wait_chip(turn + 1, False)
            self.mate_wait_chip(turn + 1, True)
        loop(self.place.half - 1, body)
        self.mate_wait_last()

    def finish(self):
        sent = self.buf.at[pl.ds(0, (4 * self.events + NP) * self.rows)]
        self.to_mate(0, sent).wait_send()


class Reduce:
    SLOTS = 4
    DEPTH = 8

    def __init__(self, place, part, shard_rows, refs):
        self.place, self.part, self.shard = place, part, shard_rows
        self.events = (place.half - 1) * NP + NP // 2
        self.ring, self.acc, self.stage, self.send_n, self.recv_n, self.send_m, self.recv_m = refs

    @staticmethod
    def scratch(half, shard_rows, width):
        events = (half - 1) * NP + NP // 2
        shapes = [(2, events), (2 * Reduce.DEPTH + NP,), (Reduce.SLOTS, 2)]
        sems = [(2, Reduce.DEPTH), (2, events), (Reduce.SLOTS,), (2 * Reduce.DEPTH + NP,)]
        return [pltpu.VMEM(s + (shard_rows, width), F32) for s in shapes] + [pltpu.SemaphoreType.DMA(s) for s in sems]

    def acc_slot(self, term):
        own = 2 * self.DEPTH + not_below_zero(term - 2 * self.events)
        return lax.select(term < 2 * self.events, lax.rem(term, 2 * self.DEPTH), own)

    def mate_copy(self, term):
        return pltpu.make_async_remote_copy(
            self.stage.at[lax.rem(term, self.SLOTS), 1 - self.place.core], self.acc.at[self.acc_slot(term)],
            self.send_m.at[lax.rem(term, self.SLOTS)], self.recv_m.at[self.acc_slot(term)], self.place.mate, MESH)

    def ring_copy(self, event, way):
        to = self.place.peer(1 - 2 * way)
        return pltpu.make_async_remote_copy(
            self.acc.at[self.acc_slot(2 * event + way)], self.ring.at[way, event],
            self.send_n.at[way, lax.rem(event, self.DEPTH)], self.recv_n.at[way, event], to, MESH)

    def fill(self, term):
        @pl.when(term >= self.SLOTS)
        def _():
            self.mate_copy(not_below_zero(term - self.SLOTS)).wait_send()
        slot = lax.rem(term, self.SLOTS)
        way = lax.rem(term, 2)

        @pl.when(term >= 2 * (self.DEPTH - 1))
        def _():
            self.ring_copy(jnp.maximum(lax.div(term, 2) - (self.DEPTH - 1), 0), way).wait_send()
        shifted = lax.div(term, 2) + NP // 2
        travels = term < 2 * self.events
        distance = not_below_zero(self.place.half - lax.div(shifted, NP))
        turn = lax.rem(shifted, NP)
        piece = lax.select(travels, lax.select(way == 0, turn, NP - 1 - turn), lax.rem(not_below_zero(term - 2 * self.events), NP))
        value = self.part(self.place.near((1 - 2 * way) * distance), piece)
        self.stage[slot, 0] = value[:self.shard]
        self.stage[slot, 1] = value[self.shard:]
        self.mate_copy(term).start()

    def event(self, event):
        def add(way):
            term = 2 * event + way
            self.mate_copy(term).wait_recv()
            slot = self.acc_slot(term)
            self.acc[slot] += self.stage[lax.rem(term, self.SLOTS), self.place.core]

            @pl.when(event >= NP)
            def _():
                before = not_below_zero(event - NP)
                self.ring_copy(before, way).wait_recv()
                self.acc[slot] += self.ring[way, before]
            self.ring_copy(event, way).start()
        loop(2, add)

    def final(self, piece):
        last = self.events - NP
        term = 2 * self.events + piece
        self.mate_copy(term).wait_recv()
        self.ring_copy(last + piece, 0).wait_recv()
        self.ring_copy(last + NP - 1 - piece, 1).wait_recv()
        return ((self.stage[term % self.SLOTS, self.place.core] + self.acc[2 * self.DEPTH + piece])
                + (self.ring[0, last + piece] + self.ring[1, last + NP - 1 - piece]))

    def finish(self):
        def across(term):
            self.mate_copy(term).wait_send()
        terms = 2 * self.events + NP
        loop_from(terms - self.SLOTS, terms, across)

        def ring(event):
            self.ring_copy(event, 0).wait_send()
            self.ring_copy(event, 1).wait_send()
        loop_from(self.events + 2 - (self.DEPTH - 1), self.events, ring)

    def run(self, filler):
        def body(turn):
            event = not_below_zero(turn - 1)
            travels = (turn >= 1) & (turn <= self.events)

            @pl.when(travels)
            def _():
                self.event(event)

            def ahead(way):
                self.fill(2 * turn + way)
            loop(2, ahead)

            @pl.when(travels)
            def _():
                filler(event)
        loop(self.events + 2, body)


def rope_pair(table):
    lanes = lax.broadcasted_iota(jnp.int32, table.shape, 1)
    swapped = pltpu.roll(table, HEAD_DIM // 2, 1)
    low = lanes < HEAD_DIM // 2
    return jnp.where(low, table, swapped), jnp.where(low, -swapped, table)


def fill_table(freqs, table_ref):
    rows = 64
    blocks = table_ref.shape[0] // rows

    def cos_sin(count, scale):
        steps = lax.broadcasted_iota(jnp.int32, (count, HEAD_DIM), 0) * scale
        angles = steps.astype(F32) * freqs
        return jnp.cos(angles), jnp.sin(angles)
    cos_low, sin_low = cos_sin(rows, 1)
    cos_high, sin_high = cos_sin(max(blocks, 8), rows)
    low = lax.broadcasted_iota(jnp.int32, (1, HEAD_DIM), 1) < HEAD_DIM // 2
    first = jnp.where(low, cos_high, sin_high)
    second = jnp.where(low, -sin_high, cos_high)
    for block in range(blocks):
        table_ref[block * rows:(block + 1) * rows] = first[block:block + 1] * cos_low + second[block:block + 1] * sin_low


def rope(values, table, inverse=False):
    cos2, sin2 = rope_pair(table)
    turned = pltpu.roll(values, HEAD_DIM // 2, 1)
    if inverse:
        return values * cos2 - turned * sin2
    return values * cos2 + turned * sin2


def norm_forward(x_f32, gain_row):
    inv = lax.rsqrt(row_mean(x_f32 * x_f32) + NORM_EPS)
    return (x_f32 * inv * gain_row).astype(BF16)


def norm_unit(x_f32):
    inv = lax.rsqrt(row_mean(x_f32 * x_f32) + NORM_EPS)
    return inv, x_f32 * inv


def norm_backward(inv, unit, gain_row, d_normed):
    d_unit = d_normed * gain_row
    return inv * (d_unit - unit * row_mean(d_unit * unit))


def by_halves(dot, a, b, axis):
    size = a.shape[axis] // 2
    first = a[:size] if axis == 0 else a[:, :size]
    second = a[size:] if axis == 0 else a[:, size:]
    return dot(first, b), dot(second, b)


def attention_block(row0, rows, keys, diagonal, refs, forward, backward):
    q_ref, k_ref, v_ref, table_ref, read_da, write_o, dx_ref, dk_ref, dv_ref = refs
    here = pl.ds(aligned(row0, rows), rows)
    scale = HEAD_DIM ** -0.5
    spans = [(start, end) for start, end in ((0, keys - diagonal), (keys - diagonal, keys)) if end > start]
    query = q_ref[here]
    scores = []
    for start, end in spans:
        part = dot_nt(query, k_ref[start:end])
        if end == keys:
            row_id = row0 - start + lax.broadcasted_iota(jnp.int32, part.shape, 0)
            part = jnp.where(row_id >= lax.broadcasted_iota(jnp.int32, part.shape, 1), part, -1e30)
        scores.append(part)
    tops = [jnp.max(part, axis=-1, keepdims=True) for part in scores]
    top = functools.reduce(jnp.maximum, tops)
    factor = scale * 1.4426950408889634
    expd = [jnp.exp2((part - top) * factor) for part in scores]
    inv_sum = 1.0 / sum(row_sum(part) for part in expd)
    prob = [part * inv_sum for part in expd]
    prob_b = [part.astype(BF16) for part in prob]
    if forward:
        halves = [by_halves(dot_nn, part, v_ref[start:end], 0) for part, (start, end) in zip(prob_b, spans)]
        out = [functools.reduce(jnp.add, [half[i] for half in halves]) for i in range(2)]
        write_o(here, jnp.concatenate(out, axis=0).astype(BF16))
    if backward:
        d_attn = read_da(here)
        d_prob = [dot_nt(d_attn, v_ref[start:end]).astype(BF16).astype(F32) for start, end in spans]
        row_dot = sum(row_sum(p * d) for p, d in zip(prob, d_prob))
        d_scores = [(p * (d - row_dot)).astype(BF16) for p, d in zip(prob, d_prob)]
        halves = [by_halves(dot_nn, part, k_ref[start:end], 0) for part, (start, end) in zip(d_scores, spans)]
        d_query = jnp.concatenate([functools.reduce(jnp.add, [half[i] for half in halves]) for i in range(2)], axis=0)
        d_query = (d_query * scale).astype(BF16).astype(F32)
        dx_ref[here, :HEAD_DIM] = rope(d_query, table_ref[here], inverse=True).astype(BF16)
        for part, prob_part, (start, end) in zip(d_scores, prob_b, spans):
            middle = (start + end) // 2
            for ref, left, right in ((dv_ref, prob_part, d_attn), (dk_ref, part, query)):
                low, high = by_halves(dot_tn, left, right, 1)
                ref[start:middle] += low
                ref[middle:end] += high


def store_keys_values(here, dx_ref, dk_ref, dv_ref, table_ref):
    d_key = (dk_ref[here] * HEAD_DIM ** -0.5).astype(BF16).astype(F32)
    dx_ref[here, HEAD_DIM:2 * HEAD_DIM] = rope(d_key, table_ref[here], inverse=True).astype(BF16)
    dx_ref[here, 2 * HEAD_DIM:3 * HEAD_DIM] = dv_ref[here].astype(BF16)


def gated_pull(gate, up, d_hidden):
    sig = jax.nn.sigmoid(gate)
    silu = gate * sig
    d_silu = d_hidden * up
    return (silu * up).astype(BF16), (d_silu * sig + d_silu * silu * (1.0 - sig)).astype(BF16), (d_hidden * silu).astype(BF16)


class Copies:
    def __init__(self, sems):
        self.sems, self.used = sems, 0

    def start(self, src, dst):
        copy = pltpu.make_async_copy(src, dst, self.take())
        copy.start()
        return copy

    def take(self):
        self.used += 1
        return self.sems.at[self.used % self.sems.shape[0]]


def gather_loop(gather, unit, then=None):
    chips = gather.place.ring

    def body(event):
        @pl.when(event < gather.events)
        def _():
            gather.event(event)
            if then is not None:
                then(event)
        step = lax.div(event, NP) + 1
        opposite = event == gather.events
        final = event == gather.events - 1
        own = event == 1
        near = (event >= NP) & (event < gather.events) & (lax.rem(event, 2) == 0)

        @pl.when(opposite)
        def _():
            gather.mate_wait_last()

        @pl.when(own | near | final)
        def _():
            gather.mate_wait_chip(step - 1, final | (lax.rem(event, NP) != 0))

        @pl.when(own | near | final | opposite)
        def _():
            distance = lax.select(opposite, gather.place.half, step - 1)
            rightward = final | (lax.rem(event, NP) != 0)
            count = lax.select(own, 0, lax.select(opposite, chips - 1, lax.select(final, chips - 2, not_below_zero(lax.div(event, 2) - 1))))
            unit(count, gather.place.near(lax.select(rightward, distance, -distance)))
    loop(gather.events + 1, body)


def weight_grads_u(block, u_ref, dx_ref, stage_ref, outs, sems, head_cols, ff):
    rows = stage_ref.shape[1]
    slot = lax.rem(block, 2)
    here = pl.ds(aligned(block * rows, rows), rows)

    def copies():
        bounds = (0, head_cols, head_cols + ff, head_cols + 2 * ff)
        return [pltpu.make_async_copy(stage_ref.at[slot, :, bounds[i]:bounds[i + 1]], outs[i].at[here], sems.at[slot, i]) for i in range(3)]

    @pl.when(block >= 2)
    def _():
        for copy in copies():
            copy.wait()
    stage_ref[slot] = dot_tn(u_ref[:, here], dx_ref[...]).astype(BF16)
    for copy in copies():
        copy.start()


def weight_grads_u_wait(stage_ref, outs, sems, head_cols, ff):
    rows = stage_ref.shape[1]
    bounds = (0, head_cols, head_cols + ff, head_cols + 2 * ff)
    for slot in range(2):
        for i in range(3):
            pltpu.make_async_copy(stage_ref.at[slot, :, bounds[i]:bounds[i + 1]], outs[i].at[pl.ds(0, rows)], sems.at[slot, i]).wait()


def weight_grads_h(piece, ho_ref, read_dy, stage_ref):
    cols = stage_ref.shape[1] // NP
    stage_ref[:, pl.ds(aligned(piece * cols, cols), cols)] = dot_tn(ho_ref[...], read_dy(piece)).astype(BF16)


def h_copies(there, stage_ref, outs, sems, ff):
    return [pltpu.make_async_copy(stage_ref.at[:HEAD_DIM, there], outs[0].at[:, there], sems.at[0]),
            pltpu.make_async_copy(stage_ref.at[HEAD_DIM:HEAD_DIM + ff, there], outs[1].at[:, there], sems.at[1])]


def kernel_main(tp_size, gain_hbm, freq_hbm, x_hbm, gy_hbm, wqkv_hbm, wout_hbm, wgate_hbm, wup_hbm, wdown_hbm,
                dx_out, gain_out, *refs):
    u_ref, g_ref, wo_ref = refs[0:3]
    lasts = refs[3:8]
    u0_hbm, q_hbm, k_hbm, v_hbm, o_hbm, ab_hbm = refs[8:14]
    (gain_ref, freq_ref, x_ref, side_ref, wc_ref, q_ref, k_ref, v_ref, ho_ref, dx_ref, dk_ref, dv_ref, table_ref, x1_ref, gs_ref,
     pair_ref, all_ref, local, sems_gs, sems_hs, sem_ps, sem_pr, sem_as, sem_ar, free_sem) = refs[14:39]
    sems_u, sems_g, refs_r = refs[39:43], refs[43:47], refs[47:]
    place = Place(tp_size)
    peers = place.arrive()
    shard, width = x_ref.shape
    pair = 2 * shard
    chips = place.ring
    head_cols = wqkv_hbm.shape[2]
    ff = wgate_hbm.shape[2]
    piece_cols = width // NP
    gate_cols = slice(head_cols, head_cols + ff)
    up_cols = slice(head_cols + ff, head_cols + 2 * ff)
    hidden_cols = slice(HEAD_DIM, HEAD_DIM + ff)
    loads = Copies(local)
    gu = Gather(place, u_ref, shard, sems_u)
    gg = Gather(place, g_ref, shard, sems_g)

    def wait_all(copies):
        for copy in copies:
            copy.wait()

    def load_wc(layer):
        return [loads.start(wqkv_hbm.at[layer], wc_ref.at[:, :head_cols]),
                loads.start(wgate_hbm.at[layer], wc_ref.at[:, gate_cols]),
                loads.start(wup_hbm.at[layer], wc_ref.at[:, up_cols])]

    def load_wo(layer):
        return [loads.start(wout_hbm.at[layer], wo_ref.at[:HEAD_DIM]), loads.start(wdown_hbm.at[layer], wo_ref.at[hidden_cols])]

    def rows_of(chip):
        return pl.ds(aligned(chip * pair, pair), pair)

    def write_o(here, value):
        ho_ref[here, :HEAD_DIM] = value

    def read_da(here):
        return dx_ref[here, :HEAD_DIM]

    def heads(here, rows_u):
        qkv = dot_nn(rows_u, wc_ref[:, :head_cols]).astype(BF16)
        table = table_ref[here]
        q_ref[here] = rope(qkv[:, :HEAD_DIM].astype(F32), table).astype(BF16)
        k_ref[here] = rope(qkv[:, HEAD_DIM:2 * HEAD_DIM].astype(F32), table).astype(BF16)
        v_ref[here] = qkv[:, 2 * HEAD_DIM:3 * HEAD_DIM]

    def forward_unit(count, chip, with_hidden):
        here = rows_of(chip)
        rows_u = u_ref[here]
        heads(here, rows_u)
        gate = dot_nn(rows_u, wc_ref[:, gate_cols]).astype(BF16)
        up = dot_nn(rows_u, wc_ref[:, up_cols]).astype(BF16)
        dx_ref[here, gate_cols] = gate
        dx_ref[here, up_cols] = up
        if with_hidden:
            gate_f, up_f = gate.astype(F32), up.astype(F32)
            ho_ref[here, hidden_cols] = (gate_f * jax.nn.sigmoid(gate_f) * up_f).astype(BF16)

    def backward_unit(count, chip):
        here = rows_of(chip)
        dah = dot_nt(g_ref[here], wo_ref[...])
        dx_ref[here, :HEAD_DIM] = dah[:, :HEAD_DIM].astype(BF16)
        d_hidden = dah[:, hidden_cols].astype(BF16).astype(F32)
        hidden, d_gate, d_up = gated_pull(dx_ref[here, gate_cols].astype(F32), dx_ref[here, up_cols].astype(F32), d_hidden)
        ho_ref[here, hidden_cols] = hidden
        dx_ref[here, gate_cols] = d_gate
        dx_ref[here, up_cols] = d_up

    def piece_of(piece):
        return pl.ds(aligned(piece * piece_cols, piece_cols), piece_cols)

    def part_forward(chip, piece):
        return dot_nn(ho_ref[rows_of(chip)], wo_ref[:, piece_of(piece)])

    def part_backward(chip, piece):
        return dot_nt(dx_ref[rows_of(chip)], wc_ref[piece_of(piece)])

    def keys_values(chip):
        store_keys_values(rows_of(chip), dx_ref, dk_ref, dv_ref, table_ref)

    def other_keys_values():
        def body(step):
            keys_values(place.near(place.half + step - chips))
        loop_from(1, chips, body)

    def read_dy(piece):
        return g_ref[:, piece_of(piece)]

    def finals(reduce):
        return jnp.concatenate([reduce.final(piece) for piece in range(NP)], axis=1)

    grad_cols = slice(head_cols + 2 * ff)
    last_u, last_h = (lasts[0], lasts[2], lasts[3]), (lasts[1], lasts[4])

    def grads_last(event):
        @pl.when(event < NP)
        def _():
            weight_grads_h(event, ho_ref, read_dy, wo_ref)
            for copy in h_copies(piece_of(event), wo_ref, last_h, sems_hs, ff):
                copy.start()

        @pl.when((event >= NP) & (event < NP + chips))
        def _():
            weight_grads_u(not_below_zero(event - NP), u_ref, dx_ref, gs_ref, last_u, sems_gs, head_cols, ff)

    def grads_last_wait():
        wait_all(h_copies(slice(None), wo_ref, last_h, sems_hs, ff))
        weight_grads_u_wait(gs_ref, last_u, sems_gs, head_cols, ff)

    def grads_first(event):
        @pl.when(event < NP)
        def _():
            weight_grads_h(event, ho_ref, read_dy, wo_ref)

        @pl.when((event >= NP) & (event < NP + chips))
        def _():
            rows = width // chips
            here = pl.ds(aligned(not_below_zero(event - NP) * rows, rows), rows)
            g_ref[here, grad_cols] = dot_tn(u_ref[:, here], dx_ref[...]).astype(BF16)

    lanes = all_ref.shape[3]
    tiles = width // lanes

    def cross(layer):
        return pltpu.make_async_remote_copy(pair_ref.at[layer, 0], pair_ref.at[layer, 1], sem_ps.at[layer], sem_pr.at[layer], place.mate, MESH)

    def spread(layer, which, step):
        part = all_ref.at[layer, which]
        return pltpu.make_async_remote_copy(part, part, sem_as.at[layer], sem_ar.at[layer], place.peer(step), MESH)

    def start_gain(layer, row):
        for tile in range(tiles):
            pair_ref[layer, 0, tile:tile + 1] = row[:, tile * lanes:(tile + 1) * lanes]
        cross(layer).start()

    def spread_gain(layer):
        cross(layer).wait()
        all_ref[layer, place.chip] = pair_ref[layer, 0] + pair_ref[layer, 1]
        for step in sorted(range(1, chips), key=lambda step: -min(step, chips - step)):
            spread(layer, place.chip, step).start()

    def end_gain(layer):
        spread(layer, slice(chips - 1), 1).wait()
        total = all_ref[layer, 0]
        for chip in range(1, chips):
            total = total + all_ref[layer, chip]
        for tile in range(tiles):
            gain_out[layer:layer + 1, tile * lanes:(tile + 1) * lanes] = total[tile:tile + 1]

    load_x = [loads.start(x_hbm, x_ref), loads.start(gain_hbm, gain_ref), loads.start(freq_hbm, freq_ref)]
    load_g = loads.start(gy_hbm, g_ref.at[gg.own_rows()])
    load_w = load_wc(0)
    load_o = load_wo(0)
    wait_all(load_x)
    u_ref[gu.own_rows()] = norm_forward(x_ref[...].astype(F32), gain_ref[0:1])
    pl.semaphore_wait(pltpu.get_barrier_semaphore(), peers)
    gu.start()
    saves = [loads.start(u_ref.at[gu.own_rows()], u0_hbm)]
    fill_table(freq_ref[:1], table_ref)
    load_g.wait()
    wait_all(load_w)

    def start_gy(event):
        @pl.when(event == gu.events - NP)
        def _():
            gg.start()
    gather_loop(gu, lambda count, chip: forward_unit(count, chip, True), start_gy)

    load_w = load_wc(1)
    saves += [loads.start(q_ref, q_hbm), loads.start(k_ref, k_hbm), loads.start(v_ref, v_hbm),
              loads.start(dx_ref.at[:, head_cols:head_cols + 2 * ff], ab_hbm)]

    def attend_first(chip):
        attention_block(chip * pair, pair, chips * pair, chips * pair, (q_ref, k_ref, v_ref, table_ref, None, write_o, None, None, None), True, False)
    attend_first(place.near(place.half))
    wait_all(load_o)
    reduce = Reduce(place, part_forward, shard, refs_r)

    def filler_forward(event):
        @pl.when(event < place.half)
        def _():
            distance = not_below_zero(place.half - 1 - event)

            def body(way):
                attend_first(place.near((1 - 2 * way) * distance))
            loop(lax.select(distance == 0, 1, 2), body)

        @pl.when(event == place.half)
        def _():
            gu.finish()
            o_copy().start()
    sem_o = loads.take()

    def o_copy():
        return pltpu.make_async_copy(ho_ref.at[:, :HEAD_DIM], o_hbm, sem_o)
    reduce.run(filler_forward)
    load_o = load_wo(1)
    gg.event(jnp.int32(0), forward=True)
    gg.event(jnp.int32(1), forward=True)
    x_next = (x_ref[...].astype(F32) + finals(reduce)).astype(BF16)
    x1_ref[...] = x_next
    saves[0].wait()
    o_copy().wait()
    u_ref[gu.own_rows()] = norm_forward(x_next.astype(F32), gain_ref[1:2])

    reduce.finish()
    gu.start()
    load_side = loads.start(u0_hbm, side_ref.at[0])
    wait_all(saves[1:])
    wait_all(load_w)
    wait_all(load_o)
    dk_ref[...] = jnp.zeros_like(dk_ref)
    dv_ref[...] = jnp.zeros_like(dv_ref)
    early = 2
    for event in range(early, NP):
        gg.event(jnp.int32(event), forward=False)

    def more_gy(event):
        first = gu.events - NP

        @pl.when((event >= first) & (event < first + NP - early))
        def _():
            gg.forward(not_below_zero(event - first) + early)

        @pl.when(event >= first + NP - early)
        def _():
            gg.event(not_below_zero(event - first) + early, forward=True)

        @pl.when((event > NP) & (event < NP + 6) & (lax.rem(event, 2) == 1))
        def _():
            turn = not_below_zero(lax.div(event - 1, 2) - 2)
            gg.mate_wait_chip(jnp.minimum(turn, 1), turn == 2)
            backward_unit(turn, place.near(lax.select(turn == 2, 1, -turn)))
    gather_loop(gu, lambda count, chip: forward_unit(count, chip, False), more_gy)

    groups = 4

    def attend_last(turn):
        held = early + NP
        distance = lax.div(turn + 1, 2)
        rightward = (turn > 0) & (lax.rem(turn, 2) == 0)
        opposite = turn == chips - 1
        needed = lax.select(turn == 0, held, lax.select(opposite, gg.events, distance * NP))
        begin = lax.select(turn == 0, held, jnp.minimum(jnp.maximum(held + turn - 1, lax.select(turn >= chips - 2, gg.events - NP // 2, 0)), gg.events))
        end = jnp.maximum(jnp.minimum(held + turn, gg.events), needed)
        end = lax.select(turn == chips - 2, jnp.maximum(end, gg.events - 1), end)
        begin = lax.select(turn == chips - 1, gg.events - 1, begin)

        @pl.when(turn == NP + 1)
        def _():
            gu.finish()
            load_side.wait()
            gu.start_side(side_ref)

        def take(event):
            gg.event(event)
        loop_from(begin, end, take)

        chip = place.near(lax.select(rightward, distance, -distance))

        @pl.when(opposite)
        def _():
            gg.mate_wait_last()

        @pl.when((turn > 2) & jnp.logical_not(opposite))
        def _():
            gg.mate_wait_chip(distance, rightward)

        @pl.when(turn > 2)
        def _():
            backward_unit(turn, chip)
        for group in range(groups):
            @pl.when(lax.div(chip, chips // groups) == group)
            def _(group=group):
                attention_block(chip * pair, pair, (group + 1) * (chips * pair // groups), chips * pair // groups,
                                (q_ref, k_ref, v_ref, table_ref, read_da, write_o, dx_ref, dk_ref, dv_ref), True, True)
    loop(chips, attend_last)
    keys_values(place.near(place.half))
    loads_a = [loads.start(q_hbm, q_ref), loads.start(k_hbm, k_ref), loads.start(v_hbm, v_ref)]
    sem_late = loads.take()

    def load_o_again():
        return pltpu.make_async_copy(o_hbm, ho_ref.at[:, :HEAD_DIM], sem_late)
    near = (place.left, place.right, place.mate)
    reduce = Reduce(place, part_backward, shard, refs_r)

    def filler_last(event):
        @pl.when(event == 0)
        def _():
            other_keys_values()
        grads_last(event)

        @pl.when(event == 1)
        def _():
            gg.finish()

        @pl.when(event == NP + chips)
        def _():
            load_o_again().start()
            for peer in near:
                pl.semaphore_signal(free_sem, inc=1, device_id=peer, device_id_type=MESH)
    reduce.run(filler_last)
    pl.semaphore_wait(free_sem, len(near))
    load_o_again().wait()
    gu.adopt_side(side_ref)
    for event in range(early):
        gu.forward_side(side_ref, event)
    d_normed = finals(reduce).astype(BF16).astype(F32)
    inv, unit = norm_unit(x1_ref[...].astype(F32))
    g_ref[gg.own_rows()] = (g_ref[gg.own_rows()].astype(F32) + norm_backward(inv, unit, gain_ref[1:2], d_normed)).astype(BF16)
    start_gain(1, jnp.sum(d_normed * unit, axis=0, keepdims=True))

    reduce.finish()
    gg.start()
    spread_gain(1)
    grads_last_wait()
    load_o = load_wo(0) + [loads.start(ab_hbm, dx_ref.at[:, head_cols:head_cols + 2 * ff])]
    load_w = load_wc(0)
    dk_ref[...] = jnp.zeros_like(dk_ref)
    dv_ref[...] = jnp.zeros_like(dv_ref)
    wait_all(load_o)

    def more_u(event):
        first = gg.events - NP

        @pl.when((event >= first) & (event < first + NP - early))
        def _():
            gu.forward_side(side_ref, not_below_zero(event - first) + early)

        @pl.when(event >= first + NP - early)
        def _():
            gu.event(not_below_zero(event - first) + early, forward=True)
    gather_loop(gg, backward_unit, more_u)
    wait_all(loads_a)

    def attend_back(block):
        @pl.when((block >= 2) & (block < gu.events - 2 * NP))
        def _():
            gu.event(block + NP, forward=True)
        for group in range(groups):
            @pl.when(lax.div(block, chips // groups) == group)
            def _(group=group):
                attention_block(block * pair, pair, (group + 1) * (chips * pair // groups), chips * pair // groups,
                                (q_ref, k_ref, v_ref, table_ref, read_da, None, dx_ref, dk_ref, dv_ref), False, True)
    loop(chips, attend_back)
    keys_values(place.near(place.half))
    wait_all(load_w)
    reduce = Reduce(place, part_backward, shard, refs_r)

    def filler_first(event):
        @pl.when(event == 0)
        def _():
            other_keys_values()

        @pl.when(event < NP)
        def _():
            gu.event(gu.events - NP + event, forward=False)

        @pl.when(event == NP - 1)
        def _():
            gu.mate_wait_all()
        grads_first(event)

        @pl.when(event == 1)
        def _():
            gg.finish()

        @pl.when(event == NP + 1)
        def _():
            gu.finish()

        @pl.when(event == NP + chips)
        def _():
            for copy in reloads():
                copy.start()
    plan = fold_plan(width, head_cols, ff)
    sems_plan = [loads.take() for part in plan]

    def reloads():
        return [pltpu.make_async_copy(lasts[number].at[theirs], u_ref.at[ours], sem) for (number, theirs, ours), sem in zip(plan, sems_plan)]
    x1_ref[...] = g_ref[gg.own_rows()]
    reduce.run(filler_first)
    inv, unit = norm_unit(x_ref[...].astype(F32))
    d_normed = finals(reduce).astype(BF16).astype(F32)
    start_gain(0, jnp.sum(d_normed * unit, axis=0, keepdims=True))
    dx_out[...] = (x1_ref[...].astype(F32) + norm_backward(inv, unit, gain_ref[0:1], d_normed)).astype(BF16)
    spread_gain(0)
    end_gain(1)
    reduce.finish()
    wait_all(reloads())
    end_gain(0)


def fold_plan(width, head_cols, ff):
    cols = head_cols + 2 * ff
    piece = width // NP
    rows = HEAD_DIM + ff
    every = slice(None)
    plan = [(0, (every, every), (every, slice(head_cols))), (2, (every, every), (every, slice(head_cols, head_cols + ff))),
            (3, (every, every), (every, slice(head_cols + ff, cols)))]
    whole = width // rows
    for turn in range(NP):
        theirs = slice(turn * piece, (turn + 1) * piece)
        if turn < whole:
            ours = slice(cols, cols + piece)
            plan += [(1, (every, theirs), (slice(turn * rows, turn * rows + HEAD_DIM), ours)),
                     (4, (every, theirs), (slice(turn * rows + HEAD_DIM, (turn + 1) * rows), ours))]
        else:
            plan += [(1, (every, theirs), (slice(whole * rows, whole * rows + HEAD_DIM), slice(cols, cols + piece)))]
            strip = width - cols - piece
            for step in range(piece // strip):
                plan += [(4, (every, slice(turn * piece + step * strip, turn * piece + (step + 1) * strip)),
                          (slice(step * ff, (step + 1) * ff), slice(cols + piece, width)))]
    return plan


def kernel_stack(head_cols, ff, last_ref, first_ref, first_h_ref, dx_ref, gain_ref, *refs):
    outs, (dx_out, gain_out, sems) = refs[0:5], refs[5:8]
    width = last_ref.shape[0]
    copies = Copies(sems)
    pending = [copies.start(dx_ref, dx_out), copies.start(gain_ref, gain_out)]
    for number, theirs, ours in fold_plan(width, head_cols, ff):
        pending.append(copies.start(last_ref.at[ours], outs[number].at[(1,) + theirs]))
    bounds = (0, head_cols, head_cols + ff, head_cols + 2 * ff)
    for i, number in enumerate((0, 2, 3)):
        pending.append(copies.start(first_ref.at[:, bounds[i]:bounds[i + 1]], outs[number].at[0]))
    pending.append(copies.start(first_h_ref.at[:HEAD_DIM], outs[1].at[0]))
    pending.append(copies.start(first_h_ref.at[HEAD_DIM:HEAD_DIM + ff], outs[4].at[0]))
    for copy in pending:
        copy.wait()


def solution(mesh):
    tp_size = mesh.shape['tp']
    half = tp_size // 4
    row_spec = P(('dp', 'tp'), None)
    col_spec = P(None, None, 'tp')
    inner_spec = P(None, 'tp', None)

    def device_program(x_loc, dy_loc, norm_gain, w_qkv, w_out, w_gate, w_up, w_down):
        shard, width = x_loc.shape
        seq = shard * tp_size
        pair = 2 * shard
        chips = tp_size // 2
        head_cols = w_qkv.shape[2]
        ff = w_gate.shape[2]
        cols = head_cols + 2 * ff
        piece_cols = width // NP
        vmem, anyspace = pl.BlockSpec(memory_space=pltpu.VMEM), pl.BlockSpec(memory_space=pl.ANY)
        shape = jax.ShapeDtypeStruct
        dma = pltpu.SemaphoreType.DMA

        freqs = np.float32(ROPE_BASE) ** (np.float32(-2.0) * np.arange(HEAD_DIM // 2, dtype=np.float32) / np.float32(HEAD_DIM))
        freqs = jnp.asarray(np.tile(freqs, (8, 2)))

        rows_shape = shape((shard, width), BF16)
        gain_shape = shape((2, width), F32)
        head_shape = shape((seq, HEAD_DIM), BF16)
        grads = (shape((width, head_cols), BF16), shape((HEAD_DIM, width), BF16), shape((width, ff), BF16),
                 shape((width, ff), BF16), shape((ff, width), BF16))
        square, folded = pltpu.VMEM((width, width), BF16), pltpu.VMEM((HEAD_DIM + ff, width), BF16)
        hbm = pl.BlockSpec(memory_space=pltpu.HBM)
        whole_vmem = 67043328
        kept = (seq * width + width * width + (HEAD_DIM + ff) * width + shard * width) * 2 + 2 ** 18
        results = pl.pallas_call(
            functools.partial(kernel_main, tp_size),
            out_shape=(pltpu.VMEM(rows_shape.shape, BF16), pltpu.VMEM(gain_shape.shape, F32), square, square, folded) + grads + (rows_shape,) + (head_shape,) * 4 + (shape((seq, 2 * ff), BF16),),
            in_specs=[hbm] * 9,
            out_specs=(vmem,) * 5 + (hbm,) * 11,
            scratch_shapes=[
                pltpu.VMEM((2, width), F32), pltpu.VMEM(freqs.shape, F32), pltpu.VMEM((shard, width), BF16),
                pltpu.VMEM((3, shard, width), BF16), pltpu.VMEM((width, cols), BF16),
                pltpu.VMEM((seq, HEAD_DIM), BF16), pltpu.VMEM((seq, HEAD_DIM), BF16), pltpu.VMEM((seq, HEAD_DIM), BF16),
                pltpu.VMEM((seq, HEAD_DIM + ff), BF16), pltpu.VMEM((seq, cols), BF16),
                pltpu.VMEM((seq, HEAD_DIM), F32), pltpu.VMEM((seq, HEAD_DIM), F32), pltpu.VMEM((seq, HEAD_DIM), F32),
                pltpu.VMEM((shard, width), BF16), pltpu.VMEM((2, width // chips, cols), BF16),
                pltpu.VMEM((2, 2, width // 128, 128), F32), pltpu.VMEM((2, chips, width // 128, 128), F32),
                dma((24,)), dma((2, 3)), dma((2,)), dma((2,)), dma((2,)), dma((2,)), dma((2,)),
                pltpu.SemaphoreType.REGULAR] + Gather.scratch(half) + Gather.scratch(half) + Reduce.scratch(half, shard, piece_cols),
            compiler_params=pltpu.CompilerParams(collective_id=1, has_side_effects=True, vmem_limit_bytes=whole_vmem - kept), name='blocks',
        )(norm_gain, freqs, x_loc, dy_loc, w_qkv, w_out, w_gate, w_up, w_down)

        stacked = pl.pallas_call(
            functools.partial(kernel_stack, head_cols, ff),
            out_shape=tuple(shape((2,) + grad.shape, BF16) for grad in grads) + (rows_shape, gain_shape),
            in_specs=[vmem] * 5,
            out_specs=(hbm,) * 7,
            scratch_shapes=[dma((1,))],
            compiler_params=pltpu.CompilerParams(vmem_limit_bytes=8 * 2 ** 20), name='stack',
        )(*results[2:5], *results[0:2])
        return tuple(stacked[5:7]) + tuple(stacked[0:5])

    return jax.shard_map(device_program, mesh=mesh, in_specs=(row_spec, row_spec, P(None, None), col_spec, inner_spec, col_spec, col_spec, inner_spec), out_specs=(row_spec, P('dp', None), P('dp', None, 'tp'), P('dp', 'tp', None), P('dp', None, 'tp'), P('dp', None, 'tp'), P('dp', 'tp', None)), check_vma=False)
```

profile of v0, /device:TPU:21, one launch (start us, length us, event | category | flops | bytes accessed | tf_op | source)
XLA Modules:
  0.0 458.9 jit_solution(8198645784040335387)
XLA Ops:
  0.6 452.0 %blocks.1 = (bf16[128,2048]{1,0:T(8,128)(2,1)S(1)}, f32[2,2048]{1,0:T(2,128)S(1)}, bf16[2048,2048]{1,0:T(8,128)(2,1)S(1)}, bf16[2048,2048]{1,0:T(8,128)(2,1)S(1)...) custom-call(f32[2,2048]{1,0:T(2,128)} %gain_hbm.1, ...), custom_call_target="tpu_custom_call" | custom-call | tf_op jit(solution)/shard_map/blocks/pallas_call | solution.py:975
  452.7 6.0 %stack.1 = (bf16[2,2048,384]{2,1,0:T(8,128)(2,1)}, bf16[2,128,2048]{2,1,0:T(8,128)(2,1)}, bf16[2,2048,512]{2,1,0:T(8,128)(2,1)}, bf16[2,2048,512]{2,1,0:T(8,128)...) custom-call(bf16[2048,2048]{1,0:T(8,128)(2,1)S(1)} %get-tuple-element.19.last_ref, ...), custom_call_target="tpu_custom_call" | custom-call | tf_op jit(solution)/shard_map/stack/pallas_call | solution.py:993
where the time goes:
time: 459 us
  Pallas kernels  458 us (100%)
    pallas_call x1, Pallas kernels, device_program(): pl.pallas_call(functools.partial(kernel_main, tp_size), out_shape=(pltpu....  452 us

commit v1 on v0

--- a/solution.py
+++ b/solution.py
@@ -116,13 +116,17 @@
     def to_mate(self, group, view):
         return self.copy(view, view, self.recv_m.at[group], self.place.mate)
 
-    def start(self):
+    def start(self, first=0):
         place = self.place
-        for piece in range(NP):
-            self.to_right(piece, self.view(place.chip, place.core, piece)).start()
-            self.to_left(piece, self.view(place.chip, place.core, NP - 1 - piece)).start()
+        for piece in range(first, NP):
+            self.start_pair(piece)
         for piece in range(NP):
             self.to_mate(0, self.view(place.chip, place.core, piece)).start()
+
+    def start_pair(self, piece):
+        place = self.place
+        self.to_right(piece, self.view(place.chip, place.core, piece)).start()
+        self.to_left(piece, self.view(place.chip, place.core, NP - 1 - piece)).start()
 
     def views(self, event):
         step = lax.div(event, NP) + 1
@@ -657,15 +661,26 @@
         for tile in range(tiles):
             gain_out[layer:layer + 1, tile * lanes:(tile + 1) * lanes] = total[tile:tile + 1]
 
-    load_x = [loads.start(x_hbm, x_ref), loads.start(gain_hbm, gain_ref), loads.start(freq_hbm, freq_ref)]
+    ends_first = sorted(range(NP), key=lambda piece: min(piece, NP - 1 - piece))
+    parts = [pl.ds(piece * gu.rows, gu.rows) for piece in ends_first]
+    load_gain = loads.start(gain_hbm, gain_ref)
+    load_x = [loads.start(x_hbm.at[part], x_ref.at[part]) for part in parts]
+    load_freq = loads.start(freq_hbm, freq_ref)
     load_g = loads.start(gy_hbm, g_ref.at[gg.own_rows()])
     load_w = load_wc(0)
     load_o = load_wo(0)
-    wait_all(load_x)
-    u_ref[gu.own_rows()] = norm_forward(x_ref[...].astype(F32), gain_ref[0:1])
-    pl.semaphore_wait(pltpu.get_barrier_semaphore(), peers)
-    gu.start()
+    load_gain.wait()
+    own_start = (place.chip * 2 + place.core) * shard
+    for turn, (piece, part) in enumerate(zip(ends_first, parts)):
+        load_x[turn].wait()
+        here = pl.ds(aligned(own_start + piece * gu.rows, gu.rows), gu.rows)
+        u_ref[here] = norm_forward(x_ref[part].astype(F32), gain_ref[0:1])
+        if turn == 1:
+            pl.semaphore_wait(pltpu.get_barrier_semaphore(), peers)
+            gu.start_pair(0)
+    gu.start(first=1)
     saves = [loads.start(u_ref.at[gu.own_rows()], u0_hbm)]
+    load_freq.wait()
     fill_table(freq_ref[:1], table_ref)
     load_g.wait()
     wait_all(load_w)
@@ -985,7 +1000,7 @@
                 pltpu.VMEM((seq, HEAD_DIM), F32), pltpu.VMEM((seq, HEAD_DIM), F32), pltpu.VMEM((seq, HEAD_DIM), F32),
                 pltpu.VMEM((shard, width), BF16), pltpu.VMEM((2, width // chips, cols), BF16),
                 pltpu.VMEM((2, 2, width // 128, 128), F32), pltpu.VMEM((2, chips, width // 128, 128), F32),
-                dma((24,)), dma((2, 3)), dma((2,)), dma((2,)), dma((2,)), dma((2,)), dma((2,)),
+                dma((16,)), dma((2, 3)), dma((2,)), dma((2,)), dma((2,)), dma((2,)), dma((2,)),
                 pltpu.SemaphoreType.REGULAR] + Gather.scratch(half) + Gather.scratch(half) + Reduce.scratch(half, shard, piece_cols),
             compiler_params=pltpu.CompilerParams(collective_id=1, has_side_effects=True, vmem_limit_bytes=whole_vmem - kept), name='blocks',
         )(norm_gain, freqs, x_loc, dy_loc, w_qkv, w_out, w_gate, w_up, w_down)

time: 459 us -> 459 us (level)
  no operation moved by 1% of the time
where the time goes in v1:
time: 459 us
  Pallas kernels  458 us (100%)
    pallas_call x1, Pallas kernels, device_program(): pl.pallas_call(functools.partial(kernel_main, tp_size), out_shape=(pltpu....  452 us

profile of v1, /device:TPU:21, one launch (start us, length us, event | category | flops | bytes accessed | tf_op | source)
XLA Modules:
  0.0 458.8 jit_solution(2636936540519012067)
XLA Ops:
  0.6 451.9 %blocks.1 = (bf16[128,2048]{1,0:T(8,128)(2,1)S(1)}, f32[2,2048]{1,0:T(2,128)S(1)}, bf16[2048,2048]{1,0:T(8,128)(2,1)S(1)}, bf16[2048,2048]{1,0:T(8,128)(2,1)S(1)...) custom-call(f32[2,2048]{1,0:T(2,128)} %gain_hbm.1, ...), custom_call_target="tpu_custom_call" | custom-call | tf_op jit(solution)/shard_map/blocks/pallas_call | solution.py:990
  452.5 6.0 %stack.1 = (bf16[2,2048,384]{2,1,0:T(8,128)(2,1)}, bf16[2,128,2048]{2,1,0:T(8,128)(2,1)}, bf16[2,2048,512]{2,1,0:T(8,128)(2,1)}, bf16[2,2048,512]{2,1,0:T(8,128)...) custom-call(bf16[2048,2048]{1,0:T(8,128)(2,1)S(1)} %get-tuple-element.19.last_ref, ...), custom_call_target="tpu_custom_call" | custom-call | tf_op jit(solution)/shard_map/stack/pallas_call | solution.py:1008

commit v2 on v1

--- a/solution.py
+++ b/solution.py
@@ -382,7 +382,7 @@
         part = dot_nt(query, k_ref[start:end])
         if end == keys:
             row_id = row0 - start + lax.broadcasted_iota(jnp.int32, part.shape, 0)
-            part = jnp.where(row_id >= lax.broadcasted_iota(jnp.int32, part.shape, 1), part, -1e30)
+            part = jnp.where(row_id >= lax.broadcasted_iota(jnp.int32, part.shape, 1), part, -1e30 / scale)
         scores.append(part)
     tops = [jnp.max(part, axis=-1, keepdims=True) for part in scores]
     top = functools.reduce(jnp.maximum, tops)
@@ -399,10 +399,10 @@
         d_attn = read_da(here)
         d_prob = [dot_nt(d_attn, v_ref[start:end]).astype(BF16).astype(F32) for start, end in spans]
         row_dot = sum(row_sum(p * d) for p, d in zip(prob, d_prob))
-        d_scores = [(p * (d - row_dot)).astype(BF16) for p, d in zip(prob, d_prob)]
+        d_scores = [(p * (d - row_dot) * scale).astype(BF16) for p, d in zip(prob, d_prob)]
         halves = [by_halves(dot_nn, part, k_ref[start:end], 0) for part, (start, end) in zip(d_scores, spans)]
         d_query = jnp.concatenate([functools.reduce(jnp.add, [half[i] for half in halves]) for i in range(2)], axis=0)
-        d_query = (d_query * scale).astype(BF16).astype(F32)
+        d_query = d_query.astype(BF16).astype(F32)
         dx_ref[here, :HEAD_DIM] = rope(d_query, table_ref[here], inverse=True).astype(BF16)
         for part, prob_part, (start, end) in zip(d_scores, prob_b, spans):
             middle = (start + end) // 2
@@ -413,7 +413,7 @@
 
 
 def store_keys_values(here, dx_ref, dk_ref, dv_ref, table_ref):
-    d_key = (dk_ref[here] * HEAD_DIM ** -0.5).astype(BF16).astype(F32)
+    d_key = dk_ref[here].astype(BF16).astype(F32)
     dx_ref[here, HEAD_DIM:2 * HEAD_DIM] = rope(d_key, table_ref[here], inverse=True).astype(BF16)
     dx_ref[here, 2 * HEAD_DIM:3 * HEAD_DIM] = dv_ref[here].astype(BF16)
 

time: 459 us -> 459 us (level)
  no operation moved by 1% of the time
where the time goes in v2:
time: 459 us
  Pallas kernels  458 us (100%)
    pallas_call x1, Pallas kernels, device_program(): pl.pallas_call(functools.partial(kernel_main, tp_size), out_shape=(pltpu....  452 us

profile of v2, /device:TPU:21, one launch (start us, length us, event | category | flops | bytes accessed | tf_op | source)
XLA Modules:
  0.0 458.9 jit_solution(11076871395332011346)
XLA Ops:
  0.6 452.0 %blocks.1 = (bf16[128,2048]{1,0:T(8,128)(2,1)S(1)}, f32[2,2048]{1,0:T(2,128)S(1)}, bf16[2048,2048]{1,0:T(8,128)(2,1)S(1)}, bf16[2048,2048]{1,0:T(8,128)(2,1)S(1)...) custom-call(f32[2,2048]{1,0:T(2,128)} %gain_hbm.1, ...), custom_call_target="tpu_custom_call" | custom-call | tf_op jit(solution)/shard_map/blocks/pallas_call | solution.py:990
  452.6 6.0 %stack.1 = (bf16[2,2048,384]{2,1,0:T(8,128)(2,1)}, bf16[2,128,2048]{2,1,0:T(8,128)(2,1)}, bf16[2,2048,512]{2,1,0:T(8,128)(2,1)}, bf16[2,2048,512]{2,1,0:T(8,128)...) custom-call(bf16[2048,2048]{1,0:T(8,128)(2,1)S(1)} %get-tuple-element.19.last_ref, ...), custom_call_target="tpu_custom_call" | custom-call | tf_op jit(solution)/shard_map/stack/pallas_call | solution.py:1008
